TPU v7x, 16 devices: a 4x2x1 block of a 4x4x8 slice. The times are simulated.
16 devices in a mesh: dp: 2 (over y, z), stage: 8 (over x, core).
Axes of the slice: x: 4, y: 2, z: 1, core: 2. Of those that a mesh axis runs over, the one named last changes fastest.
The devices are a block of a 4x4x8 slice.
Arguments:
- tokens: int32 [16, 128], P('dp'), parts along dimension 0
- labels: int32 [16, 128], P('dp'), parts along dimension 0
- emb_table: bfloat16 [32128, 512], replicated
- w_up: bfloat16 [8, 512, 2048], P('stage')
- w_down: bfloat16 [8, 2048, 512], P('stage')
Outputs:
- output 1: float32 [2], P('dp'), parts along dimension 0
- output 2: float32 [16, 512, 2048], P(('dp', 'stage')), parts along dimension 0
- output 3: float32 [16, 2048, 512], P(('dp', 'stage')), parts along dimension 0
- output 4: float32 [64256, 512], P('dp'), parts along dimension 0
There are 2 independent parts. A program takes and returns all parts, laid end to end along the dimension named above; an argument that names none is the same for every part.
All inputs are finite; a program needn't handle non-finite values.
Results may differ from a plain program's by a relative error of at most 0.02.
Values are sent between devices in bfloat16 or wider.
A program may use at most 768 MiB of HBM per device.

v0:
```python
import functools
import math

import jax
import jax.numpy as jnp
from jax import lax
from jax.experimental import pallas as pl
from jax.experimental.pallas import tpu as pltpu
from jax.sharding import PartitionSpec as P


MESH = pl.DeviceIdType.MESH
LOG2E = math.log2(math.e)
LN2 = math.log(2.0)
GELU_C = math.sqrt(2.0 / math.pi)
GELU_K = 0.044715
EPS = 1e-6
LANES = 128
F32 = jnp.float32
BF16 = jnp.bfloat16


def gelu_fwd(a):
    return (0.5 * a) * (1.0 + jnp.tanh(a * (GELU_C + (GELU_C * GELU_K) * (a * a))))


def gelu_slope(a):
    a2 = a * a
    half = 0.5 * jnp.tanh(a * (GELU_C + (GELU_C * GELU_K) * a2))
    up, down = 0.5 + half, 0.5 - half
    return up + (up * down) * (a * (2.0 * GELU_C + (6.0 * GELU_C * GELU_K) * a2))


def dot(x, y):
    return jnp.dot(x, y, preferred_element_type=F32)


def dot_t(x, y):
    return lax.dot_general(x, y, (((0,), (0,)), ((), ())), preferred_element_type=F32)


def remote(src, dst, send_sem, recv_sem, dev):
    return pltpu.make_async_remote_copy(src_ref=src, dst_ref=dst, send_sem=send_sem, recv_sem=recv_sem, device_id={"stage": dev}, device_id_type=MESH)


def column(row):
    return jnp.broadcast_to(row, (LANES, LANES)).T


def gather_kernel(ids_ref, tok_ref, emb_hbm, x0_hbm, tiles, picked, sem, out_sem):
    n_micro, seq = tok_ref.shape
    me = lax.axis_index("stage")
    group = tiles.shape[1] // seq
    slots = tiles.shape[0]
    owners = [head_chunk(me, k, n_micro) for k in range(slots)]

    def fetch(k):
        def one(i, carry):
            t = ids_ref[owners[k] * seq + i]
            start = pl.multiple_of(lax.bitwise_and(t, -group), group)
            pltpu.make_async_copy(emb_hbm.at[pl.ds(start, group)], tiles.at[k, pl.ds(pl.multiple_of(i * group, group), group)], sem.at[k]).start()
            return carry

        lax.fori_loop(0, seq, one, 0, unroll=8)

    def select(k):
        sub = lax.broadcasted_iota(jnp.int32, (LANES, LANES), 0)
        lane = lax.broadcasted_iota(jnp.int32, (LANES, LANES), 1)
        tok = column(tok_ref[pl.ds(owners[k], 1), :].astype(F32)).astype(jnp.int32)
        want = sub * group + lax.bitwise_and(tok, group - 1)
        hot = jnp.concatenate([jnp.where(lane + b * LANES == want, 1.0, 0.0).astype(BF16) for b in range(seq * group // LANES)], axis=1)
        pltpu.make_async_copy(emb_hbm.at[pl.ds(0, seq * group)], tiles.at[k], sem.at[k]).wait()
        picked[k] = dot(hot, tiles[k]).astype(BF16)
        pltpu.make_async_copy(picked.at[k], x0_hbm.at[k], out_sem.at[k]).start()

    def finish(k):
        pltpu.make_async_copy(picked.at[k], x0_hbm.at[k], out_sem.at[k]).wait()

    for work in (fetch, select, finish):
        work(0)
        for k in range(1, slots):
            pl.when(me < slots)(functools.partial(work, k))


def head_chunk(dev, k, n_micro):
    return jnp.minimum(jnp.where(dev < 2, 2 * dev + k, dev + 2), n_micro - 1)


def run_gather(tokens, emb):
    n_micro, seq = tokens.shape
    dim = emb.shape[1]
    group = 16
    return pl.pallas_call(
        gather_kernel,
        out_shape=jax.ShapeDtypeStruct((2, seq, dim), BF16),
        in_specs=[pl.BlockSpec(memory_space=pltpu.SMEM), pl.BlockSpec(memory_space=pltpu.VMEM), pl.BlockSpec(memory_space=pl.ANY)],
        out_specs=pl.BlockSpec(memory_space=pl.ANY),
        scratch_shapes=[pltpu.VMEM((2, seq * group, dim), BF16), pltpu.VMEM((2, seq, dim), BF16), pltpu.SemaphoreType.DMA((2,)), pltpu.SemaphoreType.DMA((2,))],
        cost_estimate=pl.CostEstimate(flops=10**9, bytes_accessed=2 * seq * group * dim * 2, transcendentals=0),
        name="gather",
    )(tokens.reshape(n_micro * seq), tokens, emb)


def token_table(row_ref, cut_ref, meta):
    n_tok = row_ref.shape[1]
    n_grp = n_tok // LANES
    lane = lax.broadcasted_iota(jnp.int32, (LANES, LANES), 1).astype(F32)
    sub = lax.broadcasted_iota(jnp.int32, (LANES, LANES), 0)
    row = lambda g: row_ref[:, g * LANES:(g + 1) * LANES].astype(F32)
    zero = jnp.zeros((LANES, LANES), F32)
    fold = lambda acc: jnp.sum(acc, axis=0, keepdims=True)
    cols = [column(row(c)) for c in range(n_grp)]
    firsts = []
    for g in range(n_grp):
        acc = zero
        for c in range(g + 1):
            same = cols[c] == row(g)
            if c == g:
                same = same & (sub < lane.astype(jnp.int32))
            acc = acc + jnp.where(same, 1.0, 0.0)
        firsts.append(column(jnp.where(fold(acc) == 0.0, 1.0, 0.0)))
    ranks = []
    for g in range(n_grp):
        acc = zero
        for c in range(n_grp):
            acc = acc + jnp.where(cols[c] < row(g), firsts[c], 0.0)
        ranks.append(fold(acc))
        meta[g:g + 1, :] = ranks[g].astype(jnp.int32)
    rank_cols = [column(r) for r in ranks]
    for g in range(n_grp):
        acc = zero
        for c in range(n_grp):
            acc = acc + jnp.where(rank_cols[c] == lane + g * LANES, firsts[c] * cols[c], 0.0)
        meta[n_grp + g:n_grp + g + 1, :] = fold(acc).astype(jnp.int32)
    cut = cut_ref[...].astype(F32)
    acc = zero
    for c in range(n_grp):
        acc = acc + jnp.where(cols[c] < cut, firsts[c], 0.0)
    meta[2 * n_grp:3 * n_grp, :] = jnp.broadcast_to(fold(acc), (n_grp, LANES)).astype(jnp.int32)


def logit_grad(e, n_t, shift, lab, first_id, inv_count, scale, dz):
    rows = e.shape[0]
    n_tok = n_t.shape[1]
    blk = 256
    vid = lax.broadcasted_iota(jnp.int32, (rows, blk), 0)
    for j in range(n_tok // blk):
        cols = slice(j * blk, (j + 1) * blk)
        z = (dot(e, n_t[:, cols]) * scale).astype(BF16).astype(F32)
        prob = jnp.exp2(z * LOG2E - shift[:, cols])
        dz[:, cols] = jnp.where(vid == lab[:, cols] - first_id, prob - inv_count, prob).astype(BF16)


def pipe_kernel(n_stage, plan, x0_hbm, emb_hbm, up_hbm, down_hbm, lab_hbm, row_hbm, cut_hbm,
                n_out, xs_out, hid_out, da_out, g_out, dx0_out, stat_out, loss_out, tmp_out, meta_out,
                xbuf, ybuf, abuf, hbuf, nbuf, gbuf, dxbuf, dx0buf, dnbuf, up, down, up_t, down_t,
                emb, zbuf, n_t, dn_acc, dn_send, dn_recv, dn_own, st_send, st_recv, statall, lossall, tops, n_all_t, shift, dz, obuf, z_pair, meta, lab_ref, row_ref, cut_ref,
                w_sem, e_sem, x_sem, x_send, f_send, f_recv, n_send, n_recv, nf_send, ag_send, fw_send,
                st_sems, dp_sems, dn_ssem, dn_rsem, sa_sems, lo_sems, b_send, b_recv, d_send, d_recv, r_sems, out_sem, o_sem, od_send, od_recv, ic_send, in_sem):
    n_micro, seq, dim = gbuf.shape
    part = xbuf.shape[1]
    n_part = xbuf.shape[0]
    per = seq // part
    n_tok = n_micro * seq
    ffn = up.shape[1]
    vocab = emb_hbm.shape[0]
    me = lax.axis_index("stage")
    core = lax.rem(me, 2)
    chip = me // 2
    mate = me + 1 - 2 * core
    last_id = n_stage - 1
    first = me == 0
    last = me == last_id
    fblk = 512
    n_fblk = ffn // fblk
    base, extra, tile = plan.base, plan.extra, plan.head_tile
    row0 = core * base
    n_tiles = base // tile
    wide_tile = plan.grad_tile

    barrier = pltpu.get_barrier_semaphore()
    gives_x = (me >= 1) & (me + 2 < n_micro)

    def here(dev):
        pl.semaphore_signal(barrier, inc=1, device_id={"stage": dev}, device_id_type=MESH)

    pl.when(jnp.logical_not(first))(lambda: here(me - 1))
    pl.when(jnp.logical_not(last))(lambda: here(me + 1))

    @pl.when(first)
    def _():
        for dev in range(2, n_micro - 2):
            here(dev)

    w_copy = [pltpu.make_async_copy(up_hbm, up, w_sem.at[0]), pltpu.make_async_copy(down_hbm, down, w_sem.at[1])]
    for c in w_copy:
        c.start()
    in_copy = [pltpu.make_async_copy(src, dst, in_sem.at[k]) for k, (src, dst) in enumerate(((lab_hbm, lab_ref), (row_hbm, row_ref), (cut_hbm, cut_ref)))]
    x_slots = x0_hbm.shape[0]
    x_mine = [head_chunk(me, k, n_micro) for k in range(x_slots)]

    def x_rows(m):
        return xbuf.at[pl.ds(m * per, per)]

    def x_local(k):
        return pltpu.make_async_copy(x0_hbm.at[k], x_rows(k), x_sem.at[k])

    @pl.when(first)
    def _():
        for k in range(x_slots):
            x_local(k).start()

    for c in in_copy:
        c.start()

    e_parts = plan.e_parts
    e_step = base // e_parts

    def e_copy(i):
        src = emb_hbm.at[pl.ds(pl.multiple_of(row0 + i * e_step, 16), e_step)]
        return pltpu.make_async_copy(src, emb.at[pl.ds(i * e_step, e_step)], e_sem.at[0])

    e_more = pltpu.make_async_copy(emb_hbm.at[pl.ds(2 * base, extra)], emb.at[pl.ds(base, extra)], e_sem.at[1])
    with jax.named_scope("entry"):
        pl.semaphore_wait(barrier, jnp.where(first | last, 1, 2) + jnp.where(gives_x & (me >= 2), 1, 0))

    def x_copy(k):
        return remote(x0_hbm.at[k], x_rows(x_mine[k]), x_send.at[k], f_recv.at[x_mine[k]], 0)

    @pl.when(gives_x)
    def _():
        x_copy(0).start()

        @pl.when(me < 2)
        def _():
            x_copy(1).start()

    def table_start():
        for i in range(e_parts):
            e_copy(i).start()
        pl.when(core == 1)(e_more.start)

    def transpose_weights():
        for j in range(n_fblk):
            up_t[j * fblk:(j + 1) * fblk, :] = up[:, j * fblk:(j + 1) * fblk].T
            down_t[:, j * fblk:(j + 1) * fblk] = down[j * fblk:(j + 1) * fblk, :].T

    @pl.when(jnp.logical_not(first))
    def _():
        for c in w_copy:
            c.wait()
        table_start()

    def idle_work():
        transpose_weights()
        in_copy[1].wait()
        in_copy[2].wait()
        token_table(row_ref, jnp.where(core == 0, cut_ref[0:1, :], cut_ref[1:2, :]), meta)

    @pl.when(chip >= n_stage // 4)
    def _():
        idle_work()

    def n_start(m):
        remote(nbuf.at[m], nbuf.at[m], n_send, n_recv.at[m], jnp.where(m == last_id, last_id - 1, m)).start()

    def fwd(h, carry, cold=False):
        m = h // per
        sub = lax.rem(h, per)
        rows = pl.ds(pl.multiple_of(sub * part, part), part)
        with jax.named_scope("fwd_wait"):

            @pl.when(first & (sub == 0))
            def _():
                @pl.when(m < x_slots)
                def _():
                    x_local(m).wait()

                @pl.when(m >= x_slots)
                def _():
                    remote(x_rows(m), x_rows(m), x_send.at[0], f_recv.at[m], me).wait_recv()

            @pl.when(jnp.logical_not(first))
            def _():
                remote(xbuf.at[h], xbuf.at[h], f_send, f_recv.at[h], me).wait_recv()

        with jax.named_scope("fwd_comp"):
            x = xbuf[h]
            if cold:
                w_copy[0].wait()
            for j in range(n_fblk):
                cols = slice(j * fblk, (j + 1) * fblk)
                a = dot(x, up[:, cols]).astype(BF16)
                abuf[m, rows, cols] = a
                hbuf[m, rows, cols] = gelu_fwd(a.astype(F32)).astype(BF16)
            if cold:
                w_copy[1].wait()
                table_start()
            y = (x.astype(F32) + dot(hbuf[m, rows, :], down[...])).astype(BF16)
            ybuf[h] = y

        @pl.when(jnp.logical_not(last))
        def _():
            remote(ybuf.at[h], xbuf.at[h], f_send, f_recv.at[h], me + 1).start()

        @pl.when(last)
        def _():
            yf = y.astype(F32)
            inv = lax.rsqrt(jnp.mean(yf * yf, axis=-1, keepdims=True) + EPS)
            nbuf[m, rows, :] = (yf * inv).astype(BF16)
            pl.when(sub == per - 1)(lambda: n_start(m))

        @pl.when(sub == per - 1)
        def _():
            pltpu.make_async_copy(hbuf.at[m], hid_out.at[m], out_sem.at[0]).start()
            pltpu.make_async_copy(x_rows(m), xs_out.at[pl.ds(m * per, per)], out_sem.at[1]).start()

        return carry

    pl.when(first)(lambda: (fwd(0, 0, cold=True), None)[1])
    lax.fori_loop(jnp.where(first, 1, 0), n_part, fwd, 0)

    @pl.when(chip < n_stage // 4)
    def _():
        idle_work()

    n_forward = remote(nbuf.at[me], nbuf.at[me], nf_send, n_recv.at[me], mate)
    with jax.named_scope("n_wait"):

        @pl.when(jnp.logical_not(last))
        def _():
            remote(nbuf.at[me], nbuf.at[me], n_send, n_recv.at[me], me).wait_recv()
            pl.when(mate != last_id)(n_forward.start)
            remote(nbuf.at[mate], nbuf.at[mate], n_send, n_recv.at[mate], me).wait_recv()

        for k in range(2):
            n_t[:, k * seq:(k + 1) * seq] = nbuf[2 * chip + k].T

    peers = [lax.rem(me + 2 * d, n_stage) for d in range(1, n_stage // 2)]
    ag_copies = [remote(nbuf.at[me], nbuf.at[me], ag_send.at[d], n_recv.at[me], p) for d, p in enumerate(peers)]
    for c, p in zip(ag_copies, peers):
        pl.when(p != last_id)(c.start)
    with jax.named_scope("e_wait"):
        pltpu.make_async_copy(emb_hbm.at[pl.ds(0, base)], emb.at[pl.ds(0, base)], e_sem.at[0]).wait()
        pl.when(core == 1)(e_more.wait)

    pair = 2 * seq
    scale = dim ** -0.5
    inv_count = 1.0 / n_tok
    log_count = math.log2(n_tok)
    in_copy[0].wait()
    lab = lab_ref[:, pl.ds(pl.multiple_of(chip * pair, pair), pair)]

    def logits(rows, size):
        e = emb[rows, :]
        parts = [dot(e[k * size // 2:(k + 1) * size // 2], n_t[...]) for k in range(2)]
        z = jnp.concatenate([(p * scale).astype(BF16) for p in parts], axis=0)
        zbuf[rows, :] = z
        return z

    def peak(z, size, top):
        best = jnp.max(z.reshape(size // 16, 16, pair), axis=0).astype(F32)
        return jnp.maximum(top, jnp.maximum(best[:8], best[8:]))

    def total(z, size, old, top, tot):
        off = top * LOG2E
        return tot * jnp.exp2(old * LOG2E - off) + jnp.sum(jnp.exp2(z.astype(F32).reshape(size // 8, 8, pair) * LOG2E - off[None]), axis=0)

    tops[0] = jnp.full((8, pair), -jnp.inf, F32)
    tops[1] = jnp.zeros((8, pair), F32)

    @pl.when(core == 1)
    def _():
        z = logits(pl.ds(base, extra), extra)
        top = peak(z, extra, tops[0])
        tops[1] = total(z, extra, tops[0], top, tops[1])
        tops[0] = top

    def logits_step(i, slot, old, top, tot):
        z = logits(pl.ds(pl.multiple_of(i * tile, 16), tile), tile)
        tot = total(z_pair[1 - slot], tile, old, top, tot)
        z_pair[slot] = z
        return top, peak(z, tile, top), tot

    with jax.named_scope("logits"):
        z = logits(pl.ds(0, tile), tile)
        z_pair[0] = z
        state = (tops[0], peak(z, tile, tops[0]), tops[1])
        state = lax.fori_loop(0, (n_tiles - 1) // 2, lambda i, c: logits_step(2 * i + 2, 0, *logits_step(2 * i + 1, 1, *c)), state)
        if n_tiles % 2 == 0:
            state = logits_step(n_tiles - 1, 1, *state)
        old, top, tot = state
        tot = total(z_pair[(n_tiles - 1) % 2], tile, old, top, tot)
    row_top = jnp.max(top, axis=0, keepdims=True)
    row_tot = jnp.sum(tot * jnp.exp2((top - row_top) * LOG2E), axis=0, keepdims=True)
    st_send[0:8, :] = jnp.broadcast_to(row_top, (8, pair))
    st_send[8:16, :] = jnp.broadcast_to(row_tot, (8, pair))
    st_copy = remote(st_send, st_recv, st_sems.at[0], st_sems.at[1], mate)
    with jax.named_scope("stat_x"):
        st_copy.start()
        st_copy.wait()
    far_top = st_recv[0:1, :]
    far_tot = st_recv[8:9, :]
    all_top = jnp.maximum(row_top, far_top)
    mine = row_tot * jnp.exp(row_top - all_top)
    other = far_tot * jnp.exp(far_top - all_top)
    lse = all_top + jnp.log(jnp.where(core == 0, mine + other, other + mine))
    my_shift = lse * LOG2E + log_count
    others = [lax.rem(me + d, n_stage) for d in range(1, n_stage)]

    def spread(buf, sems):
        whole = buf.at[pl.ds(0, n_stage - 1)]
        return [remote(buf.at[me], buf.at[me], sems.at[0], sems.at[1], p) for p in others], remote(whole, whole, sems.at[0], sems.at[1], me)

    statall[me] = jnp.broadcast_to(lse, (8, pair))
    sa_copies, sa_all = spread(statall, sa_sems)
    for c in sa_copies:
        c.start()

    def grads(rows, size, first_row, picked):
        zf = zbuf[rows, :].astype(F32)
        prob = jnp.exp2(zf * LOG2E - my_shift)
        hit = lax.broadcasted_iota(jnp.int32, (size, pair), 0) == lab - (row0 + first_row)
        dz_t = jnp.where(hit, prob - inv_count, prob).astype(BF16)
        got = jnp.where(hit, zf, 0.0).reshape(size // 8, 8, pair)
        return dot_t(dz_t, emb[rows, :]), picked + jnp.sum(got, axis=0)

    tops[0] = jnp.zeros((8, pair), F32)
    dn_acc[...] = jnp.zeros_like(dn_acc)

    @pl.when(core == 1)
    def _():
        dn_acc[...], tops[0] = grads(pl.ds(base, extra), extra, base, tops[0])

    def grad_step(i, picked):
        part, picked = grads(pl.ds(pl.multiple_of(i * wide_tile, 16), wide_tile), wide_tile, i * wide_tile, picked)
        dn_acc[...] += part
        return picked

    with jax.named_scope("grads"):
        picked = lax.fori_loop(0, base // wide_tile, grad_step, tops[0])
    far = pl.ds(pl.multiple_of((1 - core) * seq, seq), seq)
    near = pl.ds(pl.multiple_of(core * seq, seq), seq)
    dn_send[...] = dn_acc[far, :]
    dp_copy = remote(dn_send, dn_recv, dp_sems.at[0], dp_sems.at[1], mate)
    dp_copy.start()
    row_loss = jnp.where(core == 0, lse, 0.0) - jnp.sum(picked, axis=0, keepdims=True)
    lossall[me] = jnp.broadcast_to(row_loss, (8, pair))
    lo_copies, lo_all = spread(lossall, lo_sems)
    for c in lo_copies:
        c.start()
    with jax.named_scope("dn_x"):
        dp_copy.wait()
        dn = ((dn_acc[near, :] + dn_recv[...]) * scale).astype(BF16)
    dn_copy = remote(dn_own, dnbuf.at[me], dn_ssem, dn_rsem.at[me], last_id)

    @pl.when(last)
    def _():
        dnbuf[last_id] = dn

    @pl.when(jnp.logical_not(last))
    def _():
        dn_own[...] = dn
        remote(dn_own, dnbuf.at[me], dn_ssem, dn_rsem.at[me], last_id).start()

    with jax.named_scope("ag_wait"):
        for p in peers:
            got = remote(nbuf.at[p], nbuf.at[p], ag_send.at[0], n_recv.at[p], me)
            pl.when(jnp.logical_not(last))(got.wait_recv)
            pl.when(mate != last_id)(remote(nbuf.at[p], nbuf.at[p], fw_send, n_recv.at[p], mate).start)

    near_dst = [1, 3, last_id]
    far_dst = n_stage // 2 + 1
    direct = n_micro - 2
    by_prev = n_micro - 3
    hands_on = (core == 1) & (me != 1)

    def dx0_start(m, k, dev):
        remote(dxbuf.at[m], dx0buf.at[m], d_send.at[k], d_recv.at[m], dev).start()

    def relayed(m):
        return (m < direct) & (((me == 3) & (m != by_prev)) | (last & (m == by_prev)))

    def relay_far(m):
        remote(dx0buf.at[m], dx0buf.at[m], r_sems.at[1], d_recv.at[m], far_dst).start()

    def bwd(m):
        with jax.named_scope("bwd_wait"):
            @pl.when(jnp.logical_not(last))
            def _():
                remote(gbuf.at[m], gbuf.at[m], b_send, b_recv.at[m], me).wait_recv()

            @pl.when(last)
            def _():
                @pl.when(m != last_id)
                def _():
                    remote(dnbuf.at[m], dnbuf.at[m], dn_ssem, dn_rsem.at[m], me).wait_recv()

                yf = ybuf[pl.ds(m * per, per)].reshape(seq, dim).astype(F32)
                inv = lax.rsqrt(jnp.mean(yf * yf, axis=-1, keepdims=True) + EPS)
                dnf = dnbuf[m].astype(F32)
                proj = jnp.mean(yf * dnf, axis=-1, keepdims=True)
                gbuf[m] = (dnf * inv - yf * (inv * inv * inv * proj)).astype(BF16)

        with jax.named_scope("bwd_comp"):
            g = gbuf[m]
            for j in range(n_fblk):
                cols = slice(j * fblk, (j + 1) * fblk)
                dh = dot(g, down_t[:, cols]).astype(BF16).astype(F32)
                abuf[m, :, cols] = (dh * gelu_slope(abuf[m, :, cols].astype(F32))).astype(BF16)
            dxbuf[m] = (g.astype(F32) + dot(abuf[m], up_t[...])).astype(BF16)

        @pl.when(jnp.logical_not(first))
        def _():
            remote(dxbuf.at[m], gbuf.at[m], b_send, b_recv.at[m], me - 1).start()

        @pl.when(first)
        def _():
            pl.when(m >= direct)(lambda: dx0_start(m, len(near_dst), far_dst))
            for k, dev in enumerate(near_dst):
                dx0_start(m, k, dev)

        pltpu.make_async_copy(abuf.at[m], da_out.at[m], out_sem.at[2]).start()
        pltpu.make_async_copy(gbuf.at[m], g_out.at[m], out_sem.at[3]).start()

    n_slot = obuf.shape[0]
    busy = chip == last_id // 2
    far_tile = remote(tmp_out.at[core, pl.ds(0, plan.rows)], tmp_out.at[core, pl.ds(0, plan.rows)], ic_send, od_recv, jnp.where(first, last_id, last_id - 1))
    sends_far = first | (me == last_id - 2)

    def tile_copy(k):
        rows = pl.ds(pl.multiple_of(k * plan.rows, plan.rows), plan.rows)
        slot = lax.rem(k, n_slot)
        return pltpu.make_async_copy(obuf.at[slot], tmp_out.at[core, rows], o_sem.at[slot])

    def piece(p):
        k = p // plan.per_tile
        rows = pl.ds(pl.multiple_of(p * plan.piece, plan.piece), plan.piece)
        here = pl.ds(pl.multiple_of(lax.rem(p, plan.per_tile) * plan.piece, plan.piece), plan.piece)
        return remote(obuf.at[lax.rem(k, n_slot), here], tmp_out.at[core, rows], od_send.at[k], od_recv, mate)

    def tile_sent(k):
        slot = lax.rem(k, n_slot)
        return remote(obuf.at[slot], tmp_out.at[core, pl.ds(0, plan.rows)], od_send.at[k], od_recv, mate)

    def emb_tile(k):
        with jax.named_scope("tile_prep"):

            @pl.when(k == 0)
            def _():
                for d in range(1, n_stage // 2):
                    src = lax.rem(mate + 2 * d, n_stage)
                    pl.when(jnp.logical_not(last))(remote(nbuf.at[src], nbuf.at[src], ag_send.at[0], n_recv.at[src], me).wait_recv)
                for m in range(n_micro):
                    n_all_t[:, m * seq:(m + 1) * seq] = nbuf[m].T
                sa_all.wait_recv()
                for c in range(n_stage // 2):
                    shift[:, c * pair:(c + 1) * pair] = statall[2 * c, 0:1, :] * LOG2E + log_count

        slot = lax.rem(k, n_slot)
        with jax.named_scope("tile_wait"):
            @pl.when(k == 2)
            def _():
                tile_copy(0).wait()
                pl.when(sends_far)(far_tile.start)

            pl.when(k > n_slot)(lambda: tile_copy(k - n_slot).wait())
            pl.when((k >= n_slot) & (k - n_slot < plan.shared) & jnp.logical_not(busy & (k == n_slot)))(lambda: tile_sent(k - n_slot).wait_send())

        with jax.named_scope("tile"):
            rows = pl.ds(pl.multiple_of(k * plan.rows, plan.rows), plan.rows)
            logit_grad(emb[rows, :], n_all_t, shift, lab_ref, row0 + k * plan.rows, inv_count, scale, dz)
            obuf[slot] = dot(dz[...], nbuf[...].reshape(n_tok, dim)) * scale

        tile_copy(k).start()

    def send_pieces(done, until):
        lax.fori_loop(done, until, lambda p, c: (piece(p).start(), c)[1], 0)

    def send_tiles(done, until):
        def one(k, carry):
            rows = pl.ds(pl.multiple_of(k * plan.rows, plan.rows), plan.rows)
            remote(obuf.at[lax.rem(k, n_slot)], tmp_out.at[core, rows], od_send.at[k], od_recv, mate).start()
            return carry

        lax.fori_loop(done, until, one, 0)

    before = sum(jnp.where(me == s, plan.before[s], 0) for s in range(n_stage))

    def pass_dx0(m, carry):
        @pl.when(jnp.logical_not(first))
        def _():
            remote(dx0buf.at[m], dx0buf.at[m], r_sems.at[0], d_recv.at[m], me).wait_recv()

            @pl.when(hands_on)
            def _():
                remote(dx0buf.at[m], dx0buf.at[m], r_sems.at[0], d_recv.at[m], mate).start()

            @pl.when(relayed(m))
            def _():
                relay_far(m)

            pltpu.make_async_copy(dx0buf.at[m], dx0_out.at[m], out_sem.at[4]).start()

        @pl.when(first)
        def _():
            pltpu.make_async_copy(dxbuf.at[m], dx0_out.at[m], out_sem.at[4]).start()

        return carry

    lead = jnp.where(me == 3, -300, jnp.where(last, -1800, jnp.where(me == far_dst, -1600, -10**6)))

    def work(i, carry):
        sent, passed = carry
        chunk = (i >= before) & (i < before + n_micro)
        pl.when(chunk)(lambda: bwd(i - before))
        k = jnp.where(i < before, i, i - n_micro)
        pl.when(jnp.logical_not(chunk))(lambda: emb_tile(k))
        after = i - before - n_micro + 1
        here = jnp.where(after > 0, jnp.clip((after * 264 + lead) // 138, 0, n_micro), 0)
        lax.fori_loop(passed, here, pass_dx0, 0)
        ready = jnp.where(i < before, i + 1, jnp.where(chunk, before, i + 1 - n_micro))
        near_chunks = chunk | ((i < before) & (i + jnp.where(before >= 6, 2, 1) >= before))
        whole = (sent + plan.per_tile - 1) // plan.per_tile
        upto = jnp.minimum(jnp.minimum(ready, plan.shared), whole + 1)
        some = jnp.where(near_chunks, jnp.minimum(sent + 1, jnp.minimum(ready, plan.shared) * plan.per_tile), whole * plan.per_tile)
        send_pieces(sent, some)
        send_tiles(whole, jnp.where(near_chunks, 0, upto))
        now = jnp.where(near_chunks, some, jnp.maximum(some, upto * plan.per_tile))
        return jnp.maximum(sent, now), jnp.maximum(passed, here)

    sent, passed = lax.fori_loop(0, plan.tiles + n_micro, work, (jnp.where(busy, plan.per_tile, 0), 0))
    outs = [pltpu.make_async_copy(nbuf, n_out, out_sem.at[5]), pltpu.make_async_copy(lossall, loss_out, out_sem.at[6]), pltpu.make_async_copy(meta, meta_out, out_sem.at[7])]
    lo_all.wait_recv()
    for c in outs:
        c.start()
    pltpu.make_async_copy(statall, stat_out, out_sem.at[8]).start()
    with jax.named_scope("relay_all"):
        lax.fori_loop(passed, n_micro, pass_dx0, 0)

    with jax.named_scope("drain"):
        send_pieces(sent, plan.shared * plan.per_tile)
        for k in range(max(plan.tiles - n_slot, 0), plan.tiles):
            tile_copy(k).wait()
            if k < plan.shared:
                tile_sent(k).wait_send()
        pl.when(sends_far)(far_tile.wait_send)
        all_rows = pl.ds(0, plan.shared * plan.rows)
        remote(tmp_out.at[1 - core, all_rows], tmp_out.at[1 - core, all_rows], od_send.at[0], od_recv, me).wait_recv()
        sa_all.wait_send()
        lo_all.wait_send()
        pltpu.make_async_copy(statall, stat_out, out_sem.at[8]).wait()
        for c, p in zip(ag_copies, peers):
            pl.when(p != last_id)(c.wait_send)

        @pl.when(jnp.logical_not(last))
        def _():
            dn_copy.wait_send()
            pl.when(mate != last_id)(n_forward.wait_send)
            remote(ybuf, xbuf, f_send, f_recv.at[0], me + 1).wait_send()

        @pl.when(last)
        def _():
            remote(nbuf, nbuf, n_send, n_recv.at[0], me).wait_send()

        @pl.when(mate != last_id)
        def _():
            some = nbuf.at[pl.ds(0, len(peers))]
            remote(some, some, fw_send, n_recv.at[0], mate).wait_send()

        @pl.when(gives_x)
        def _():
            x_copy(0).wait_send()

            @pl.when(me < 2)
            def _():
                x_copy(1).wait_send()

        @pl.when(jnp.logical_not(first))
        def _():
            remote(dxbuf, gbuf, b_send, b_recv.at[0], me).wait_send()
            pl.when(hands_on)(remote(dx0buf, dx0buf, r_sems.at[0], d_recv.at[0], mate).wait_send)

        @pl.when(first)
        def _():
            for k in range(len(near_dst)):
                remote(dxbuf, dx0buf, d_send.at[k], d_recv.at[0], me).wait_send()
            rest = pl.ds(0, n_micro - direct)
            remote(dxbuf.at[rest], dx0buf.at[rest], d_send.at[len(near_dst)], d_recv.at[0], me).wait_send()

        for dev, kept in ((3, direct - 1), (last_id, 1)):
            some = dx0buf.at[pl.ds(0, kept)]
            pl.when(me == dev)(remote(some, some, r_sems.at[1], d_recv.at[0], me).wait_send)

        pltpu.make_async_copy(hbuf, hid_out, out_sem.at[0]).wait()
        pltpu.make_async_copy(xbuf, xs_out, out_sem.at[1]).wait()
        pltpu.make_async_copy(abuf, da_out, out_sem.at[2]).wait()
        pltpu.make_async_copy(gbuf, g_out, out_sem.at[3]).wait()
        pltpu.make_async_copy(dx0buf, dx0_out, out_sem.at[4]).wait()
        for c in outs:
            c.wait()


class Plan:
    def __init__(self, vocab, n_stage):
        units = vocab // LANES
        self.base = units // 2 * LANES
        self.extra = vocab - 2 * self.base
        self.head_tile = next(t for t in (1600, 1536, 1280, 1024, 768, 640, 512, 256, 128) if self.base % t == 0)
        self.rows = 1024
        self.tiles, self.shared = 11, 9
        self.grad_tile = next(t for t in (4000, 3200, 1600, 1280, 640, 256, 128) if self.base % t == 0)
        self.e_parts = next(k for k in (10, 8, 5, 4, 2, 1) if self.base % (16 * k) == 0)
        self.part = 128
        self.slots = 4
        self.piece = 256
        self.per_tile = self.rows // self.piece
        measured = [10, 9, 6, 5, 3, 2, 0, 0]
        self.before = (measured + [0] * n_stage)[:n_stage]
        mid = self.base
        ends = [(0, mid), (mid, vocab)]
        early = (self.tiles * self.rows, self.shared * self.rows)
        self.spans = [[(ends[h][0] + early[0 if h == c else 1], ends[h][1]) for h in (c, 1 - c)] for c in range(2)]
        self.longest = [max(self.spans[c][k][1] - self.spans[c][k][0] for c in range(2)) for k in range(2)]
        best = min(range(16, 1281, 16), key=lambda r: (sum(-(-n // r) for n in self.longest)) * (r + 40))
        self.calc_rows = best
        self.calc_steps = [-(-n // best) for n in self.longest]
        self.steps = sum(self.calc_steps)
        self.copy_rows = self.rows
        self.copies = self.tiles + self.shared
        self.starts = ends

    def calc_start(self, core, s):
        k = 0 if s < self.calc_steps[0] else 1
        lo, hi = self.spans[core][k]
        return min(lo + (s - k * self.calc_steps[0]) * self.calc_rows, hi - self.calc_rows)

    def copy_start(self, core, c):
        own = c < self.tiles
        h = core if own else 1 - core
        return self.starts[h][0] + (c if own else c - self.tiles) * self.copy_rows

    def cuts(self, core):
        firsts = [(self.calc_start(core, s), self.calc_rows) for s in range(self.steps)] + [(self.copy_start(core, c), self.copy_rows) for c in range(self.copies)]
        flat = [v for lo, rows in firsts for v in (lo, lo + rows)]
        return flat + [0] * (LANES - len(flat))


def run_pipe(x0, emb, w_up, w_down, labels, tokens, cuts, n_stage, plan):
    n_micro, seq = labels.shape
    dim, ffn = w_up.shape
    n_tok = n_micro * seq
    base = plan.base
    any_spec = pl.BlockSpec(memory_space=pl.ANY)
    act = (n_micro, seq, dim)
    fine = (n_tok // plan.part, plan.part, dim)
    wide = (n_micro, seq, ffn)
    dma = pltpu.SemaphoreType.DMA
    vm = pltpu.VMEM
    pair = 2 * seq
    return pl.pallas_call(
        functools.partial(pipe_kernel, n_stage, plan),
        out_shape=[
            jax.ShapeDtypeStruct(act, BF16), jax.ShapeDtypeStruct(fine, BF16), jax.ShapeDtypeStruct(wide, BF16),
            jax.ShapeDtypeStruct(wide, BF16), jax.ShapeDtypeStruct(act, BF16), jax.ShapeDtypeStruct(act, BF16),
            jax.ShapeDtypeStruct((n_stage, 8, pair), F32), jax.ShapeDtypeStruct((n_stage, 8, pair), F32), jax.ShapeDtypeStruct((2, plan.tiles * plan.rows, dim), F32),
            jax.ShapeDtypeStruct((3 * n_tok // LANES, LANES), jnp.int32),
        ],
        in_specs=[any_spec] * 7,
        out_specs=[any_spec] * 10,
        scratch_shapes=[
            vm(fine, BF16), vm(fine, BF16), vm(wide, BF16), vm(wide, BF16), vm(act, BF16), vm(act, BF16), vm(act, BF16), vm(act, BF16), vm(act, BF16),
            vm((dim, ffn), BF16), vm((ffn, dim), BF16), vm((ffn, dim), BF16), vm((dim, ffn), BF16),
            vm((base + plan.extra, dim), BF16), vm((base + plan.extra, pair), BF16), vm((dim, pair), BF16), vm((pair, dim), F32),
            vm((seq, dim), F32), vm((seq, dim), F32), vm((seq, dim), BF16), vm((16, pair), F32), vm((16, pair), F32), vm((n_stage, 8, pair), F32), vm((n_stage, 8, pair), F32),
            vm((2, 8, pair), F32), vm((dim, n_tok), BF16), vm((1, n_tok), F32), vm((plan.rows, n_tok), BF16), vm((plan.slots, plan.rows, dim), F32),
            vm((2, plan.head_tile, pair), BF16), vm((3 * n_tok // LANES, LANES), jnp.int32),
            vm((1, n_tok), jnp.int32), vm((1, n_tok), jnp.int32), vm((2, LANES), jnp.int32),
            dma((2,)), dma((2,)), dma((2,)), dma((2,)), dma, dma((n_tok // plan.part,)), dma, dma((n_micro,)), dma,
            dma((n_stage // 2,)), dma,
            dma((2,)), dma((2,)), dma, dma((n_stage,)), dma((2,)), dma((2,)), dma, dma((n_micro,)), dma((4,)), dma((n_micro,)), dma((2,)), dma((9,)),
            dma((plan.slots,)), dma((plan.shared,)), dma, dma, dma((3,)),
        ],
        compiler_params=pltpu.CompilerParams(collective_id=0, has_side_effects=True, vmem_limit_bytes=67_000_000),
        cost_estimate=pl.CostEstimate(flops=60 * 10**9, bytes_accessed=100 * 10**6, transcendentals=0),
        name="pipe",
    )(x0.reshape(x0.shape[0], seq // plan.part, plan.part, dim), emb, w_up, w_down, labels.reshape(1, n_tok), tokens.reshape(1, n_tok), cuts)


def fin_kernel(n_stage, n_tok, plan, ids_hbm, emb_hbm, tmp_hbm, n_hbm, stat_hbm, part_hbm, lab_hbm, meta_hbm, dx0_hbm, xs_hbm, hid_hbm, da_hbm, g_hbm,
               out_hbm, loss_ref, gup_hbm, gdown_hbm,
               n_all, dx0, xs, hid, da, g, n_t, x_t, dx0s, dz, shift, e_in, c_out, cp, gup, gdown,
               ld_sem, e_sem, t_sem, co_sem, po_sem, gu_sem, gd_sem, wi_sem, ids_ref, stat_ref, part_ref, lab_ref, meta_ref, in_sem):
    dim, ffn = gup_hbm.shape
    scale = dim ** -0.5
    inv_count = 1.0 / n_tok
    steps, crows, prows = plan.steps, plan.calc_rows, plan.copy_rows
    core = lax.rem(lax.axis_index("stage"), 2)
    early = plan.tiles * prows
    wblk = gup.shape[2]
    n_wblk = ffn // wblk
    turn = plan.calc_steps[0]

    def pick(pair):
        return jnp.where(core == 0, pair[0], pair[1])

    def calc_start(s):
        own = s < turn
        lo, hi = [jnp.where(own, pick([plan.spans[c][0][e] for c in range(2)]), pick([plan.spans[c][1][e] for c in range(2)])) for e in range(2)]
        return pl.multiple_of(jnp.minimum(lo + (s - jnp.where(own, 0, turn)) * crows, hi - crows), 16)

    def copy_start(c):
        own = c < plan.tiles
        first = jnp.where(own, pick([plan.starts[0][0], plan.starts[1][0]]), pick([plan.starts[1][0], plan.starts[0][0]]))
        return pl.multiple_of(first + (c - jnp.where(own, 0, plan.tiles)) * prows, 16)

    def e_copy(s):
        return pltpu.make_async_copy(emb_hbm.at[pl.ds(calc_start(s), crows)], e_in.at[lax.rem(s, 3)], e_sem.at[lax.rem(s, 3)])

    n_slot = cp.shape[0]
    ahead = 8

    def t_copy(c):
        own = c < plan.tiles
        row = jnp.where(own, core, 1 - core) * early + (c - jnp.where(own, 0, plan.tiles)) * prows
        slot = lax.rem(c, n_slot)
        return pltpu.make_async_copy(tmp_hbm.at[pl.ds(pl.multiple_of(row, 16), prows)], cp.at[slot], t_sem.at[slot])

    def p_out(c):
        slot = lax.rem(c, n_slot)
        return pltpu.make_async_copy(cp.at[slot], out_hbm.at[pl.ds(copy_start(c), prows)], po_sem.at[slot])

    def c_outs(s):
        slot = lax.rem(s, 2)
        return pltpu.make_async_copy(c_out.at[slot], out_hbm.at[pl.ds(calc_start(s), crows)], co_sem.at[slot])

    loads = [pltpu.make_async_copy(s, d, ld_sem.at[i]) for i, (s, d) in enumerate(((n_hbm, n_all), (dx0_hbm, dx0), (xs_hbm, xs), (g_hbm, g)))]
    ins = [pltpu.make_async_copy(s, d, in_sem.at[i]) for i, (s, d) in enumerate(((stat_hbm, stat_ref), (lab_hbm, lab_ref), (part_hbm, part_ref), (meta_hbm, meta_ref), (ids_hbm, ids_ref)))]
    loads[0].start()
    ins[0].start()
    ins[1].start()
    e_copy(0).start()
    loads[1].start()
    for c in ins[2:]:
        c.start()
    e_copy(1).start()
    for c in range(ahead):
        t_copy(c).start(priority=1)
    pair = stat_ref.shape[2]
    with jax.named_scope("fin_pre"):
        ins[0].wait()
        ins[1].wait()
        for c in range(n_stage // 2):
            shift[:, c * pair:(c + 1) * pair] = stat_ref[2 * c, 0:1, :] * LOG2E + math.log2(n_tok)
        loads[0].wait()
        n_t[...] = n_all[...].T

    def sum_rows():
        for c in ins[2:]:
            c.wait()
        loss_ref[0] = jnp.sum(sum(part_ref[d, 0:1, :] for d in range(n_stage))) * inv_count
        loads[1].wait()
        dense = jnp.concatenate([meta_ref[g:g + 1, :] for g in range(n_tok // LANES)], axis=1)
        order = lax.broadcasted_iota(jnp.int32, (n_tok, n_tok), 0) == dense
        dx0s[...] = dot(jnp.where(order, 1.0, 0.0).astype(BF16), dx0[...])

    def add_rows(k, start, ref):
        lo, hi = ids_ref[2 * n_tok + k], ids_ref[2 * n_tok + k + 1]
        wide = 8

        def some(p, width):
            at = [pl.ds(ids_ref[n_tok + p + u] - start, 1) for u in range(width)]
            new = [ref[at[u], :] + dx0s[pl.ds(p + u, 1), :] for u in range(width)]
            for u in range(width):
                ref[at[u], :] = new[u]

        def group(g, carry):
            some(lo + g * wide, wide)
            return carry

        def single(p, carry):
            some(p, 1)
            return carry

        n_grp = (hi - lo) // wide
        lax.fori_loop(0, n_grp, group, 0)
        lax.fori_loop(lo + n_grp * wide, hi, single, 0)

    def w_ins(w):
        cols = pl.ds(pl.multiple_of(w * wblk, wblk), wblk)
        wslot = lax.rem(w, 2)
        return (pltpu.make_async_copy(da_hbm.at[:, cols], da.at[wslot], wi_sem.at[0, wslot]), pltpu.make_async_copy(hid_hbm.at[:, cols], hid.at[wslot], wi_sem.at[1, wslot]))

    def w_outs(w):
        cols = pl.ds(pl.multiple_of(w * wblk, wblk), wblk)
        wslot = lax.rem(w, 2)
        return (pltpu.make_async_copy(gup.at[wslot], gup_hbm.at[:, cols], gu_sem.at[wslot]), pltpu.make_async_copy(gdown.at[wslot], gdown_hbm.at[cols], gd_sem.at[wslot]))

    def copy_tile(c, carry):
        with jax.named_scope("copy_wait"):
            t_copy(c).wait()
        with jax.named_scope("add_p"):
            add_rows(2 * steps + 2 * c, copy_start(c), cp.at[lax.rem(c, n_slot)])
        p_out(c).start()

        @pl.when(c + ahead < plan.copies)
        def _():
            pl.when(c + ahead >= n_slot)(lambda: p_out(c + ahead - n_slot).wait())
            t_copy(c + ahead).start(priority=1)

        return carry

    w_first = 2
    tails = [turn - 1, steps - 1]

    def tail(s):
        return (s == tails[0]) | (s == tails[1])

    def step(s, carry):
        pl.when(s + 2 < steps)(lambda: e_copy(s + 2).start())
        with jax.named_scope("fin_wait"):
            e_copy(s).wait()

        @pl.when(s == 0)
        def _():
            for c in loads[2:]:
                c.start()

        w = s - w_first

        @pl.when((w + 1 >= 0) & (w + 1 < n_wblk))
        def _():
            for c in w_ins(w + 1):
                c.start()

        pl.when((s >= 2) & jnp.logical_not(tail(s - 1)))(lambda: c_outs(s - 2).wait())
        slot = lax.rem(s, 2)
        start = calc_start(s)
        with jax.named_scope("calc"):
            logit_grad(e_in[lax.rem(s, 3)], n_t, shift, lab_ref, start, inv_count, scale, dz)
            c_out[slot] = dot(dz[...], n_all[...]) * scale
        pl.when(s == 0)(sum_rows)
        with jax.named_scope("add_c"):
            add_rows(2 * s, start, c_out.at[slot])
        pl.when(tail(s))(lambda: c_outs(s - 1).wait())
        c_outs(s).start()
        lax.fori_loop(s * plan.copies // (steps - 1), jnp.minimum((s + 1) * plan.copies // (steps - 1), plan.copies), copy_tile, 0)

        @pl.when(w == 0)
        def _():
            for c in loads[2:]:
                c.wait()
            x_t[...] = xs[...].T

        @pl.when((w >= 0) & (w < n_wblk))
        def _():
            wslot = lax.rem(w, 2)
            with jax.named_scope("dw_wait"):
                for c in w_ins(w):
                    c.wait()

                @pl.when(w >= 2)
                def _():
                    for c in w_outs(w - 2):
                        c.wait()

            with jax.named_scope("dw"):
                gup[wslot] = dot(x_t[...], da[wslot])
                gdown[wslot] = dot_t(hid[wslot], g[...])
            for c in w_outs(w):
                c.start()

        return carry

    lax.fori_loop(0, steps, step, 0)
    with jax.named_scope("fin_drain"):
        for w in range(n_wblk - 2, n_wblk):
            for c in w_outs(w):
                c.wait()
        c_outs(steps - 1).wait()
        for c in range(plan.copies - n_slot, plan.copies):
            p_out(c).wait()


def run_fin(emb, tmp, n_all, stats, losses, labels, meta, dx0, xs, hid, da, g, n_stage, plan):
    vocab, dim = emb.shape
    n_tok, ffn = hid.shape
    vm = pltpu.VMEM
    dma = pltpu.SemaphoreType.DMA
    any_spec = pl.BlockSpec(memory_space=pl.ANY)
    smem = pl.BlockSpec(memory_space=pltpu.SMEM)
    wblk = 512
    return pl.pallas_call(
        functools.partial(fin_kernel, n_stage, n_tok, plan),
        out_shape=[jax.ShapeDtypeStruct((vocab, dim), F32), jax.ShapeDtypeStruct((1,), F32), jax.ShapeDtypeStruct((dim, ffn), F32), jax.ShapeDtypeStruct((ffn, dim), F32)],
        in_specs=[any_spec] * 13,
        out_specs=[any_spec, smem, any_spec, any_spec],
        scratch_shapes=[
            vm((n_tok, dim), BF16), vm((n_tok, dim), BF16), vm((n_tok, dim), BF16), vm((2, n_tok, wblk), BF16), vm((2, n_tok, wblk), BF16), vm((n_tok, dim), BF16),
            vm((dim, n_tok), BF16), vm((dim, n_tok), BF16), vm((n_tok, dim), F32), vm((plan.calc_rows, n_tok), BF16), vm((1, n_tok), F32),
            vm((3, plan.calc_rows, dim), BF16), vm((2, plan.calc_rows, dim), F32), vm((11, plan.copy_rows, dim), F32),
            vm((2, dim, wblk), F32), vm((2, wblk, dim), F32),
            dma((4,)), dma((3,)), dma((11,)), dma((2,)), dma((11,)), dma((2,)), dma((2,)), dma((2, 2)),
            pltpu.SMEM((meta.size,), jnp.int32), vm(stats.shape, F32), vm(losses.shape, F32), vm((1, n_tok), jnp.int32), vm(meta.shape, jnp.int32), dma((5,)),
        ],
        compiler_params=pltpu.CompilerParams(vmem_limit_bytes=67_000_000),
        cost_estimate=pl.CostEstimate(flops=2 * n_tok * vocab * dim, bytes_accessed=5 * vocab * dim, transcendentals=0),
        name="fin",
    )(meta.reshape(-1), emb, tmp, n_all, stats, losses, labels.reshape(1, n_tok), meta, dx0, xs, hid, da, g)


def solution(mesh):
    n_stage = mesh.shape["stage"]

    def device_fn(tokens, labels, emb, w_up, w_down):
        n_micro, seq = tokens.shape
        vocab, dim = emb.shape
        w_up, w_down = w_up[0], w_down[0]
        n_tok = n_micro * seq
        plan = Plan(vocab, n_stage)
        cuts = jnp.array([plan.cuts(0), plan.cuts(1)], jnp.int32)
        x0 = run_gather(tokens, emb)
        n_all, xs, hid, da, g, dx0, stats, losses, tmp, meta = run_pipe(x0, emb, w_up, w_down, labels, tokens, cuts, n_stage, plan)
        flat = lambda p: p.reshape(n_tok, -1)
        grad_emb, loss, grad_up, grad_down = run_fin(
            emb, tmp.reshape(-1, dim), flat(n_all), stats, losses, labels, meta, flat(dx0), flat(xs), flat(hid), flat(da), flat(g), n_stage, plan
        )
        return loss, grad_up[None], grad_down[None], grad_emb

    return jax.shard_map(device_fn, mesh=mesh, in_specs=(P("dp", None), P("dp", None), P(None, None), P("stage", None, None), P("stage", None, None)), out_specs=(P("dp"), P(("dp", "stage"), None, None), P(("dp", "stage"), None, None), P("dp", None)), check_vma=False)
```

profile of v0, /device:TPU:125, one launch (start us, length us, event | category | flops | bytes accessed | tf_op | source)
XLA Modules:
  0.0 154.2 jit_solution(16243738522527695646)
XLA Ops:
  0.6 3.6 %gather.1 = bf16[2,128,512]{2,1,0:T(8,128)(2,1)} custom-call(s32[1024]{0:T(1024)} %bitcast.17, s32[8,128]{1,0:T(8,128)} %tok_ref.1, bf16[32128,512]{1,0:T(8,128)(2,1)} %emb_hbm.5), custom_call_target="tpu_custom_call" | custom-call | flops 1000000000 | bytes 4194304 | tf_op jit(solution)/shard_map/gather/pallas_call | solution.py:93
  4.2 100.8 %pipe.1 = (bf16[8,128,512]{2,1,0:T(8,128)(2,1)}, bf16[8,128,512]{2,1,0:T(8,128)(2,1)}, bf16[8,128,2048]{2,1,0:T(8,128)(2,1)}, bf16[8,128,2048]{2,1,0:T(8,128)(2,...) custom-call(bf16[2,1,128,512]{3,2,1,0:T(8,128)(2,1)} %bitcast.16, ...), custom_call_target="tpu_custom_call" | custom-call | flops 60000002048 | bytes 100000000 | tf_op jit(solution)/shard_map/pipe/pallas_call | solution.py:761
  105.0 49.0 %fin.1 = (f32[32128,512]{1,0:T(8,128)}, f32[1]{0:T(128)}, f32[512,2048]{1,0:T(8,128)}, f32[2048,512]{1,0:T(8,128)}) custom-call(s32[3072]{0:T(1024)} %bitcast.32, bf16[32128,512]{1,0:T(8,128)(2,1)} %emb_hbm.5, f32[22528,512]{1,0:T(8,128)} %bitcast.23, bf16[1024,512]{1,0:T(8,128)(2,1)} %bitcast.28, f32[8,8,256]{2,1,0:T(8,128)} %get-tuple-element.21.stat_hbm, ...), custom_call_target="tpu_custom_call" | custom-call | flops 33688649728 | bytes 82247680 | tf_op jit(solution)/shard_map/fin/pallas_call | solution.py:993
where the time goes:
time: 154 us
  Pallas kernels  153 us (99%)
    pallas_call x1, Pallas kernels, run_pipe(): pl.pallas_call(functools.partial(pipe_kernel, n_stage, plan), out_shape=[...  101 us
    pallas_call x1, Pallas kernels, run_fin(): pl.pallas_call(functools.partial(fin_kernel, n_stage, n_tok, plan), out_s...  49 us
    pallas_call x1, Pallas kernels, run_gather(): pl.pallas_call(gather_kernel, out_shape=jax.ShapeDtypeStruct((2, seq, dim...  3.56 us

commit v1 on v0

--- a/solution.py
+++ b/solution.py
@@ -152,7 +152,7 @@
 
 
 def pipe_kernel(n_stage, plan, x0_hbm, emb_hbm, up_hbm, down_hbm, lab_hbm, row_hbm, cut_hbm,
-                n_out, xs_out, hid_out, da_out, g_out, dx0_out, stat_out, loss_out, tmp_out, meta_out,
+                n_out, xs_out, hid_out, da_out, g_out, dx0_out, stat_out, loss_out, tmp_out, meta_out, nt_out,
                 xbuf, ybuf, abuf, hbuf, nbuf, gbuf, dxbuf, dx0buf, dnbuf, up, down, up_t, down_t,
                 emb, zbuf, n_t, dn_acc, dn_send, dn_recv, dn_own, st_send, st_recv, statall, lossall, tops, n_all_t, shift, dz, obuf, z_pair, meta, lab_ref, row_ref, cut_ref,
                 w_sem, e_sem, x_sem, x_send, f_send, f_recv, n_send, n_recv, nf_send, ag_send, fw_send,
@@ -398,6 +398,10 @@
     st_copy = remote(st_send, st_recv, st_sems.at[0], st_sems.at[1], mate)
     with jax.named_scope("stat_x"):
         st_copy.start()
+        for p in peers:
+            got = remote(nbuf.at[p], nbuf.at[p], ag_send.at[0], n_recv.at[p], me)
+            pl.when(jnp.logical_not(last))(got.wait_recv)
+            pl.when(mate != last_id)(remote(nbuf.at[p], nbuf.at[p], fw_send, n_recv.at[p], mate).start)
         st_copy.wait()
     far_top = st_recv[0:1, :]
     far_tot = st_recv[8:9, :]
@@ -450,6 +454,13 @@
     for c in lo_copies:
         c.start()
     with jax.named_scope("dn_x"):
+        for d in range(1, n_stage // 2):
+            src = lax.rem(mate + 2 * d, n_stage)
+            pl.when(jnp.logical_not(last))(remote(nbuf.at[src], nbuf.at[src], ag_send.at[0], n_recv.at[src], me).wait_recv)
+        for m in range(n_micro):
+            n_all_t[:, m * seq:(m + 1) * seq] = nbuf[m].T
+        nt_copy = pltpu.make_async_copy(n_all_t, nt_out, out_sem.at[9])
+        nt_copy.start()
         dp_copy.wait()
         dn = ((dn_acc[near, :] + dn_recv[...]) * scale).astype(BF16)
     dn_copy = remote(dn_own, dnbuf.at[me], dn_ssem, dn_rsem.at[me], last_id)
@@ -462,12 +473,6 @@
     def _():
         dn_own[...] = dn
         remote(dn_own, dnbuf.at[me], dn_ssem, dn_rsem.at[me], last_id).start()
-
-    with jax.named_scope("ag_wait"):
-        for p in peers:
-            got = remote(nbuf.at[p], nbuf.at[p], ag_send.at[0], n_recv.at[p], me)
-            pl.when(jnp.logical_not(last))(got.wait_recv)
-            pl.when(mate != last_id)(remote(nbuf.at[p], nbuf.at[p], fw_send, n_recv.at[p], mate).start)
 
     near_dst = [1, 3, last_id]
     far_dst = n_stage // 2 + 1
@@ -548,11 +553,6 @@
 
             @pl.when(k == 0)
             def _():
-                for d in range(1, n_stage // 2):
-                    src = lax.rem(mate + 2 * d, n_stage)
-                    pl.when(jnp.logical_not(last))(remote(nbuf.at[src], nbuf.at[src], ag_send.at[0], n_recv.at[src], me).wait_recv)
-                for m in range(n_micro):
-                    n_all_t[:, m * seq:(m + 1) * seq] = nbuf[m].T
                 sa_all.wait_recv()
                 for c in range(n_stage // 2):
                     shift[:, c * pair:(c + 1) * pair] = statall[2 * c, 0:1, :] * LOG2E + log_count
@@ -697,6 +697,7 @@
         pltpu.make_async_copy(abuf, da_out, out_sem.at[2]).wait()
         pltpu.make_async_copy(gbuf, g_out, out_sem.at[3]).wait()
         pltpu.make_async_copy(dx0buf, dx0_out, out_sem.at[4]).wait()
+        nt_copy.wait()
         for c in outs:
             c.wait()
 
@@ -764,10 +765,10 @@
             jax.ShapeDtypeStruct(act, BF16), jax.ShapeDtypeStruct(fine, BF16), jax.ShapeDtypeStruct(wide, BF16),
             jax.ShapeDtypeStruct(wide, BF16), jax.ShapeDtypeStruct(act, BF16), jax.ShapeDtypeStruct(act, BF16),
             jax.ShapeDtypeStruct((n_stage, 8, pair), F32), jax.ShapeDtypeStruct((n_stage, 8, pair), F32), jax.ShapeDtypeStruct((2, plan.tiles * plan.rows, dim), F32),
-            jax.ShapeDtypeStruct((3 * n_tok // LANES, LANES), jnp.int32),
+            jax.ShapeDtypeStruct((3 * n_tok // LANES, LANES), jnp.int32), jax.ShapeDtypeStruct((dim, n_tok), BF16),
         ],
         in_specs=[any_spec] * 7,
-        out_specs=[any_spec] * 10,
+        out_specs=[any_spec] * 11,
         scratch_shapes=[
             vm(fine, BF16), vm(fine, BF16), vm(wide, BF16), vm(wide, BF16), vm(act, BF16), vm(act, BF16), vm(act, BF16), vm(act, BF16), vm(act, BF16),
             vm((dim, ffn), BF16), vm((ffn, dim), BF16), vm((ffn, dim), BF16), vm((dim, ffn), BF16),
@@ -778,7 +779,7 @@
             vm((1, n_tok), jnp.int32), vm((1, n_tok), jnp.int32), vm((2, LANES), jnp.int32),
             dma((2,)), dma((2,)), dma((2,)), dma((2,)), dma, dma((n_tok // plan.part,)), dma, dma((n_micro,)), dma,
             dma((n_stage // 2,)), dma,
-            dma((2,)), dma((2,)), dma, dma((n_stage,)), dma((2,)), dma((2,)), dma, dma((n_micro,)), dma((4,)), dma((n_micro,)), dma((2,)), dma((9,)),
+            dma((2,)), dma((2,)), dma, dma((n_stage,)), dma((2,)), dma((2,)), dma, dma((n_micro,)), dma((4,)), dma((n_micro,)), dma((2,)), dma((10,)),
             dma((plan.slots,)), dma((plan.shared,)), dma, dma, dma((3,)),
         ],
         compiler_params=pltpu.CompilerParams(collective_id=0, has_side_effects=True, vmem_limit_bytes=67_000_000),
@@ -787,7 +788,7 @@
     )(x0.reshape(x0.shape[0], seq // plan.part, plan.part, dim), emb, w_up, w_down, labels.reshape(1, n_tok), tokens.reshape(1, n_tok), cuts)
 
 
-def fin_kernel(n_stage, n_tok, plan, ids_hbm, emb_hbm, tmp_hbm, n_hbm, stat_hbm, part_hbm, lab_hbm, meta_hbm, dx0_hbm, xs_hbm, hid_hbm, da_hbm, g_hbm,
+def fin_kernel(n_stage, n_tok, plan, ids_hbm, emb_hbm, tmp_hbm, n_hbm, nt_hbm, stat_hbm, part_hbm, lab_hbm, meta_hbm, dx0_hbm, xs_hbm, hid_hbm, da_hbm, g_hbm,
                out_hbm, loss_ref, gup_hbm, gdown_hbm,
                n_all, dx0, xs, hid, da, g, n_t, x_t, dx0s, dz, shift, e_in, c_out, cp, gup, gdown,
                ld_sem, e_sem, t_sem, co_sem, po_sem, gu_sem, gd_sem, wi_sem, ids_ref, stat_ref, part_ref, lab_ref, meta_ref, in_sem):
@@ -836,10 +837,12 @@
 
     loads = [pltpu.make_async_copy(s, d, ld_sem.at[i]) for i, (s, d) in enumerate(((n_hbm, n_all), (dx0_hbm, dx0), (xs_hbm, xs), (g_hbm, g)))]
     ins = [pltpu.make_async_copy(s, d, in_sem.at[i]) for i, (s, d) in enumerate(((stat_hbm, stat_ref), (lab_hbm, lab_ref), (part_hbm, part_ref), (meta_hbm, meta_ref), (ids_hbm, ids_ref)))]
-    loads[0].start()
+    nt_load = pltpu.make_async_copy(nt_hbm, n_t, in_sem.at[5])
+    nt_load.start()
     ins[0].start()
     ins[1].start()
     e_copy(0).start()
+    loads[0].start()
     loads[1].start()
     for c in ins[2:]:
         c.start()
@@ -852,8 +855,8 @@
         ins[1].wait()
         for c in range(n_stage // 2):
             shift[:, c * pair:(c + 1) * pair] = stat_ref[2 * c, 0:1, :] * LOG2E + math.log2(n_tok)
+        nt_load.wait()
         loads[0].wait()
-        n_t[...] = n_all[...].T
 
     def sum_rows():
         for c in ins[2:]:
@@ -982,7 +985,7 @@
             p_out(c).wait()
 
 
-def run_fin(emb, tmp, n_all, stats, losses, labels, meta, dx0, xs, hid, da, g, n_stage, plan):
+def run_fin(emb, tmp, n_all, n_all_t, stats, losses, labels, meta, dx0, xs, hid, da, g, n_stage, plan):
     vocab, dim = emb.shape
     n_tok, ffn = hid.shape
     vm = pltpu.VMEM
@@ -993,7 +996,7 @@
     return pl.pallas_call(
         functools.partial(fin_kernel, n_stage, n_tok, plan),
         out_shape=[jax.ShapeDtypeStruct((vocab, dim), F32), jax.ShapeDtypeStruct((1,), F32), jax.ShapeDtypeStruct((dim, ffn), F32), jax.ShapeDtypeStruct((ffn, dim), F32)],
-        in_specs=[any_spec] * 13,
+        in_specs=[any_spec] * 14,
         out_specs=[any_spec, smem, any_spec, any_spec],
         scratch_shapes=[
             vm((n_tok, dim), BF16), vm((n_tok, dim), BF16), vm((n_tok, dim), BF16), vm((2, n_tok, wblk), BF16), vm((2, n_tok, wblk), BF16), vm((n_tok, dim), BF16),
@@ -1001,12 +1004,12 @@
             vm((3, plan.calc_rows, dim), BF16), vm((2, plan.calc_rows, dim), F32), vm((11, plan.copy_rows, dim), F32),
             vm((2, dim, wblk), F32), vm((2, wblk, dim), F32),
             dma((4,)), dma((3,)), dma((11,)), dma((2,)), dma((11,)), dma((2,)), dma((2,)), dma((2, 2)),
-            pltpu.SMEM((meta.size,), jnp.int32), vm(stats.shape, F32), vm(losses.shape, F32), vm((1, n_tok), jnp.int32), vm(meta.shape, jnp.int32), dma((5,)),
+            pltpu.SMEM((meta.size,), jnp.int32), vm(stats.shape, F32), vm(losses.shape, F32), vm((1, n_tok), jnp.int32), vm(meta.shape, jnp.int32), dma((6,)),
         ],
         compiler_params=pltpu.CompilerParams(vmem_limit_bytes=67_000_000),
         cost_estimate=pl.CostEstimate(flops=2 * n_tok * vocab * dim, bytes_accessed=5 * vocab * dim, transcendentals=0),
         name="fin",
-    )(meta.reshape(-1), emb, tmp, n_all, stats, losses, labels.reshape(1, n_tok), meta, dx0, xs, hid, da, g)
+    )(meta.reshape(-1), emb, tmp, n_all, n_all_t, stats, losses, labels.reshape(1, n_tok), meta, dx0, xs, hid, da, g)
 
 
 def solution(mesh):
@@ -1020,10 +1023,10 @@
         plan = Plan(vocab, n_stage)
         cuts = jnp.array([plan.cuts(0), plan.cuts(1)], jnp.int32)
         x0 = run_gather(tokens, emb)
-        n_all, xs, hid, da, g, dx0, stats, losses, tmp, meta = run_pipe(x0, emb, w_up, w_down, labels, tokens, cuts, n_stage, plan)
+        n_all, xs, hid, da, g, dx0, stats, losses, tmp, meta, n_all_t = run_pipe(x0, emb, w_up, w_down, labels, tokens, cuts, n_stage, plan)
         flat = lambda p: p.reshape(n_tok, -1)
         grad_emb, loss, grad_up, grad_down = run_fin(
-            emb, tmp.reshape(-1, dim), flat(n_all), stats, losses, labels, meta, flat(dx0), flat(xs), flat(hid), flat(da), flat(g), n_stage, plan
+            emb, tmp.reshape(-1, dim), flat(n_all), n_all_t, stats, losses, labels, meta, flat(dx0), flat(xs), flat(hid), flat(da), flat(g), n_stage, plan
         )
         return loss, grad_up[None], grad_down[None], grad_emb
 

time: 154 us -> 160 us (1.039)
  Pallas kernels: 153 us -> 159 us
    pallas_call x1, Pallas kernels: 101 us -> 106 us  [run_pipe(): pl.pallas_call(functools.partial(pipe_kernel, n_stage, plan), out_shape=[...]
where the time goes in v1:
time: 160 us
  Pallas kernels  159 us (99%)
    pallas_call x1, Pallas kernels, run_pipe(): pl.pallas_call(functools.partial(pipe_kernel, n_stage, plan), out_shape=[...  106 us
    pallas_call x1, Pallas kernels, run_fin(): pl.pallas_call(functools.partial(fin_kernel, n_stage, n_tok, plan), out_s...  49.4 us
    pallas_call x1, Pallas kernels, run_gather(): pl.pallas_call(gather_kernel, out_shape=jax.ShapeDtypeStruct((2, seq, dim...  3.6 us

profile of v1, /device:TPU:125, one launch (start us, length us, event | category | flops | bytes accessed | tf_op | source)
XLA Modules:
  0.0 160.1 jit_solution(1387518188562564263)
XLA Ops:
  0.6 3.6 %gather.1 = bf16[2,128,512]{2,1,0:T(8,128)(2,1)} custom-call(s32[1024]{0:T(1024)} %bitcast.17, s32[8,128]{1,0:T(8,128)} %tok_ref.1, bf16[32128,512]{1,0:T(8,128)(2,1)} %emb_hbm.5), custom_call_target="tpu_custom_call" | custom-call | flops 1000000000 | bytes 4194304 | tf_op jit(solution)/shard_map/gather/pallas_call | solution.py:93
  4.2 106.2 %pipe.1 = (bf16[8,128,512]{2,1,0:T(8,128)(2,1)}, bf16[8,128,512]{2,1,0:T(8,128)(2,1)}, bf16[8,128,2048]{2,1,0:T(8,128)(2,1)}, bf16[8,128,2048]{2,1,0:T(8,128)(2,...) custom-call(bf16[2,1,128,512]{3,2,1,0:T(8,128)(2,1)} %bitcast.16, ...), custom_call_target="tpu_custom_call" | custom-call | flops 60000002048 | bytes 100000000 | tf_op jit(solution)/shard_map/pipe/pallas_call | solution.py:762
  110.5 49.4 %fin.1 = (f32[32128,512]{1,0:T(8,128)}, f32[1]{0:T(128)}, f32[512,2048]{1,0:T(8,128)}, f32[2048,512]{1,0:T(8,128)}) custom-call(s32[3072]{0:T(1024)} %bitcast.32, bf16[32128,512]{1,0:T(8,128)(2,1)} %emb_hbm.5, f32[22528,512]{1,0:T(8,128)} %bitcast.23, bf16[1024,512]{1,0:T(8,128)(2,1)} %bitcast.28, bf16[512,1024]{1,0:T(8,128)(2,1)} %get-tuple-element.22.nt_hbm, ...), custom_call_target="tpu_custom_call" | custom-call | flops 33688649728 | bytes 82247680 | tf_op jit(solution)/shard_map/fin/pallas_call | solution.py:996

commit v2 on v0

--- a/solution.py
+++ b/solution.py
@@ -608,7 +608,7 @@
 
         return carry
 
-    lead = jnp.where(me == 3, -300, jnp.where(last, -1800, jnp.where(me == far_dst, -1600, -10**6)))
+    lead = jnp.where(me == 3, -300, jnp.where(last, -1800, jnp.where(me == far_dst, -1750, -10**6)))
 
     def work(i, carry):
         sent, passed = carry

time: 154 us -> 154 us (level)
  no operation moved by 1% of the time
where the time goes in v2:
time: 154 us
  Pallas kernels  154 us (100%)
    pallas_call x1, Pallas kernels, run_pipe(): pl.pallas_call(functools.partial(pipe_kernel, n_stage, plan), out_shape=[...  101 us
    pallas_call x1, Pallas kernels, run_fin(): pl.pallas_call(functools.partial(fin_kernel, n_stage, n_tok, plan), out_s...  49.2 us
    pallas_call x1, Pallas kernels, run_gather(): pl.pallas_call(gather_kernel, out_shape=jax.ShapeDtypeStruct((2, seq, dim...  3.49 us

profile of v2, /device:TPU:125, one launch (start us, length us, event | category | flops | bytes accessed | tf_op | source)
XLA Modules:
  0.0 154.4 jit_solution(67612872634465901)
XLA Ops:
  0.6 3.5 %gather.1 = bf16[2,128,512]{2,1,0:T(8,128)(2,1)} custom-call(s32[1024]{0:T(1024)} %bitcast.17, s32[8,128]{1,0:T(8,128)} %tok_ref.1, bf16[32128,512]{1,0:T(8,128)(2,1)} %emb_hbm.5), custom_call_target="tpu_custom_call" | custom-call | flops 1000000000 | bytes 4194304 | tf_op jit(solution)/shard_map/gather/pallas_call | solution.py:93
  4.1 100.9 %pipe.1 = (bf16[8,128,512]{2,1,0:T(8,128)(2,1)}, bf16[8,128,512]{2,1,0:T(8,128)(2,1)}, bf16[8,128,2048]{2,1,0:T(8,128)(2,1)}, bf16[8,128,2048]{2,1,0:T(8,128)(2,...) custom-call(bf16[2,1,128,512]{3,2,1,0:T(8,128)(2,1)} %bitcast.16, ...), custom_call_target="tpu_custom_call" | custom-call | flops 60000002048 | bytes 100000000 | tf_op jit(solution)/shard_map/pipe/pallas_call | solution.py:761
  105.0 49.2 %fin.1 = (f32[32128,512]{1,0:T(8,128)}, f32[1]{0:T(128)}, f32[512,2048]{1,0:T(8,128)}, f32[2048,512]{1,0:T(8,128)}) custom-call(s32[3072]{0:T(1024)} %bitcast.32, bf16[32128,512]{1,0:T(8,128)(2,1)} %emb_hbm.5, f32[22528,512]{1,0:T(8,128)} %bitcast.23, bf16[1024,512]{1,0:T(8,128)(2,1)} %bitcast.28, f32[8,8,256]{2,1,0:T(8,128)} %get-tuple-element.21.stat_hbm, ...), custom_call_target="tpu_custom_call" | custom-call | flops 33688649728 | bytes 82247680 | tf_op jit(solution)/shard_map/fin/pallas_call | solution.py:993
